TPU v7x, 32 devices: a whole 2x2x4 slice. The times are simulated.
32 devices in a mesh: inst: 4 (over x, core), dp: 4 (over z), tp: 2 (over y).
Axes of the slice: x: 2, y: 2, z: 4, core: 2. Of those that a mesh axis runs over, the one named last changes fastest.
Arguments:
- kernel_grads: bfloat16 [16, 2, 128, 4608], P(('inst', 'dp'), 'tp'), may hold values from -0.75 to 0.75
- kernel_master: float32 [2, 128, 4608], P('tp', 'dp'), may hold values from -6 to 6
- kernel_first: float32 [2, 128, 4608], P('tp', 'dp'), may hold values from -3 to 3
- kernel_second: float32 [2, 128, 4608], P('tp', 'dp'), may hold values from 0.05 to 4
- gain_grads: bfloat16 [32, 4, 4608], P(('inst', 'dp', 'tp')), may hold values from -0.29882812 to 0.29882812
- gain_master: float32 [4, 4608], replicated, may hold values from -6 to 6
- gain_first: float32 [4, 4608], replicated, may hold values from -3 to 3
- gain_second: float32 [4, 4608], replicated, may hold values from 0.05 to 4
Outputs:
- kernel_params: bfloat16 [2, 128, 4608], P('tp')
- kernel_master_new: float32 [2, 128, 4608], P('tp', 'dp')
- kernel_first_new: float32 [2, 128, 4608], P('tp', 'dp')
- kernel_second_new: float32 [2, 128, 4608], P('tp', 'dp')
- gain_params: bfloat16 [4, 4608], replicated
- gain_master_new: float32 [4, 4608], replicated
- gain_first_new: float32 [4, 4608], replicated
- gain_second_new: float32 [4, 4608], replicated
All inputs are finite; a program needn't handle non-finite values.
Results may differ from a plain program's by a relative error of at most 0.004.
Values may be sent and summed in bfloat16 or wider, within the bound.
A program may use at most 64 MiB of HBM per device.

v0:
```python
import jax
import jax.numpy as jnp
from jax import lax
from jax.sharding import PartitionSpec as P

beta_one = 0.9
beta_two = 0.95
learn_rate = 0.01
decay_rate = 0.1
epsilon = 1e-08
step_count = 100.0


def adam_update(gradient, master, first_moment, second_moment):
    first_next = beta_one * first_moment + (1.0 - beta_one) * gradient
    second_next = beta_two * second_moment + (1.0 - beta_two) * gradient * gradient
    first_hat = first_next / (1.0 - beta_one**step_count)
    second_hat = second_next / (1.0 - beta_two**step_count)
    master_next = master - learn_rate * (
        first_hat / (jnp.sqrt(second_hat) + epsilon) + decay_rate * master
    )
    return (master_next, first_next, second_next)


def local(
    kernel_grads,
    kernel_master,
    kernel_first,
    kernel_second,
    gain_grads,
    gain_master,
    gain_first,
    gain_second,
):
    local_grads = kernel_grads[0].astype(jnp.float32)
    gain_local = gain_grads[0].astype(jnp.float32)
    flat_grads = gain_local.reshape(-1)
    gain_whole = None
    partial_rows, gain_piece = (
        lax.psum_scatter(
            local_grads.astype(jnp.bfloat16), "dp", scatter_dimension=1, tiled=True
        ).astype(jnp.float32),
        lax.psum_scatter(
            flat_grads.astype(jnp.bfloat16), "dp", scatter_dimension=0, tiled=True
        ).astype(jnp.float32),
    )
    gradient, gain_piece = (
        lax.psum(partial_rows.astype(jnp.bfloat16), "inst").astype(jnp.float32),
        lax.psum(gain_piece.astype(jnp.bfloat16), "inst").astype(jnp.float32),
    )
    kernel_master_new, kernel_first_new, kernel_second_new = adam_update(
        gradient, kernel_master, kernel_first, kernel_second
    )
    kernel_params = lax.all_gather(kernel_master_new.astype(jnp.bfloat16), "dp", axis=1, tiled=True)
    gain_piece = lax.psum(gain_piece, "tp")
    gain_whole = lax.all_gather(gain_piece, "dp", axis=0, tiled=True).reshape(gain_master.shape)
    gain_master_new, gain_first_new, gain_second_new = adam_update(
        gain_whole, gain_master, gain_first, gain_second
    )
    gain_params = gain_master_new.astype(jnp.bfloat16)
    return (
        kernel_params,
        kernel_master_new,
        kernel_first_new,
        kernel_second_new,
        gain_params,
        gain_master_new,
        gain_first_new,
        gain_second_new,
    )


def solution(mesh):
    return jax.shard_map(
        local,
        mesh=mesh,
        in_specs=(
            P(("inst", "dp"), "tp", None, None),
            P("tp", "dp", None),
            P("tp", "dp", None),
            P("tp", "dp", None),
            P(("inst", "dp", "tp"), None, None),
            P(),
            P(),
            P(),
        ),
        out_specs=(
            P("tp", None, None),
            P("tp", "dp", None),
            P("tp", "dp", None),
            P("tp", "dp", None),
            P(),
            P(),
            P(),
            P(),
        ),
        check_vma=False,
    )
```

profile of v0, /device:TPU:0, one launch (start us, length us, event | category | flops | bytes accessed | tf_op | source)
XLA Modules:
  0.0 142.5 jit_solution(16182226304347898728)
XLA Ops:
  7.2 0.0 copy-start.1
  7.2 0.0 copy-start
  7.2 0.0 reduce-scatter.2.cloned.1.call-start
  7.2 0.7 reduce-scatter.2.cloned.1.call-update
  7.9 0.0 all-reduce.3.cloned.1.call-start
  8.0 34.4 %reduce-scatter.2.cloned.1.call-done = bf16[1,32,4608]{2,1,0:T(8,128)(2,1)} async-done(((bf16[1,128,4608]{2,1,0:T(8,128)(2,1)}), bf16[1,32,4608]{2,1,0:T(8,128)(2,1)}) %reduce-scatter.2.cloned.1.call-update) | async-done | bytes 294928 | tf_op jit(solution)/shard_map/reduce_scatter | solution.py:40
  42.4 0.0 all-reduce.3.cloned.1.call-update
  42.4 0.0 copy-start.5
  42.4 0.0 copy-start.6
  42.4 0.0 copy-start.2
  42.5 0.0 all-gather.3.cloned.1.call-start
  42.5 33.3 %all-reduce.3.cloned.1.call-done = bf16[1,32,4608]{2,1,0:T(8,128)(2,1)} async-done(((bf16[1,32,4608]{2,1,0:T(8,128)(2,1)}), bf16[1,32,4608]{2,1,0:T(8,128)(2,1)}) %all-reduce.3.cloned.1.call-update) | async-done | bytes 294928 | tf_op jit(solution)/shard_map/psum | solution.py:48
  75.8 0.0 copy-done
  75.8 2.7 %fusion.7 = (bf16[1,32,4608]{2,1,0:T(8,128)(2,1)}, f32[1,32,4608]{2,1,0:T(8,128)}, f32[1,32,4608]{2,1,0:T(8,128)}, f32[1,32,4608]{2,1,0:T(8,128)}) fusion(f32[1,32,4608]{2,1,0:T(8,128)S(1)} %copy-done, bf16[1,32,4608]{2,1,0:T(8,128)(2,1)} %all-reduce.3.cloned.1.call-done, f32[1,32,4608]{2,1,0:T(8,128)S(1)} %copy-done.1, f32[1,32,4608]{2,1,0:T(8,128)} %param.11), kind=kLoop, calls=%fused_computation.11 | loop fusion | flops 2506752 | bytes 4128768 | tf_op jit(solution)/shard_map/convert_element_type | solution.py:54
  78.5 0.0 all-gather.3.cloned.1.call-update
  78.6 0.6 dynamic-slice
  79.9 20.5 %all-reduce = bf16[18432]{0:T(1024)(128)(2,1)S(1)} all-reduce(bf16[18432]{0:T(1024)(128)(2,1)S(1)} %squeeze.7), channel_id=3, replica_groups=mesh['inst'=4,'dp'=4,'tp'=2] {'dp'}, use_global_device_ids=true, to_apply=%region_2.0.clone | all-reduce | flops 18432 | bytes 73728
  100.4 0.1 dynamic-slice.1
  100.5 10.9 %psum.22 = bf16[4608]{0:T(1024)(128)(2,1)S(1)} all-reduce(bf16[4608]{0:T(1024)(128)(2,1)S(1)} %dynamic-slice.1), channel_id=1, replica_groups=mesh['inst'=4,'dp'=4,'tp'=2] {'inst'}, use_global_device_ids=true, to_apply=%region_3.0 | all-reduce | flops 4608 | bytes 18432 | tf_op jit(solution)/shard_map/psum | solution.py:49
  111.4 8.2 %psum.23 = f32[4608]{0:T(1024)S(1)} all-reduce(bf16[4608]{0:T(1024)(128)(2,1)S(1)} %psum.22), channel_id=1, replica_groups=mesh['inst'=4,'dp'=4,'tp'=2] {'tp'}, use_global_device_ids=true, to_apply=%region_4.0 | all-reduce | flops 4608 | bytes 27648 | tf_op jit(solution)/shard_map/psum | solution.py:55
  119.6 13.2 %all-gather = f32[4,1,4608]{2,1,0:T(1,128)S(1)} all-gather(f32[1,1,4608]{2,1,0:T(1,128)S(1)} %reshape.22), channel_id=1, replica_groups=mesh['inst'=4,'dp'=4,'tp'=2] {'dp'}, dimensions={0}, use_global_device_ids=true | all-gather | bytes 92160 | tf_op jit(solution)/shard_map/all_gather | solution.py:56
  132.8 0.0 copy-done.4
  132.8 0.8 fusion.4
  133.6 2.4 %copy.23 = bf16[1,128,4608]{2,1,0:T(8,128)(2,1)} copy(bf16[1,128,4608]{2,1,0:T(8,128)(2,1)} %all-gather.3.cloned.1.call-done) | data formatting | bytes 2359296
  (10 shorter events, 0.0 us)
Async XLA Ops:
  7.2 68.6 %copy-start.1 = (f32[1,32,4608]{2,1,0:T(8,128)S(1)}, f32[1,32,4608]{2,1,0:T(8,128)}, u32[]{:S(2)}) copy-start(f32[1,32,4608]{2,1,0:T(8,128)} %param.10) | copy-start | bytes 1769476
  7.2 68.6 %copy-start = (f32[1,32,4608]{2,1,0:T(8,128)S(1)}, f32[1,32,4608]{2,1,0:T(8,128)}, u32[]{:S(2)}) copy-start(f32[1,32,4608]{2,1,0:T(8,128)} %param.9) | copy-start | bytes 1769476
  7.2 35.2 %reduce-scatter.2.cloned.1.call-start = ((), (), s32[]{:S(2)}) async-start(), calls=%async_computation.1 | async-start | bytes 1474560 | tf_op jit(solution)/shard_map/reduce_scatter | solution.py:40
  7.9 67.9 %all-reduce.3.cloned.1.call-start = ((), (), s32[]{:S(2)}) async-start(), calls=%async_computation.2 | async-start | bytes 589824 | tf_op jit(solution)/shard_map/psum | solution.py:48
  42.4 36.2 %copy-start.5 = (bf16[1,4,4608]{2,1,0:T(4,128)(2,1)S(1)}, bf16[1,4,4608]{2,1,0:T(4,128)(2,1)}, u32[]{:S(2)}) copy-start(bf16[1,4,4608]{2,1,0:T(4,128)(2,1)} %param.12) | copy-start | bytes 110596
  42.4 36.2 %copy-start.6 = (u32[32]{0:T(128)S(1)}, u32[32]{0:T(128)}, u32[]{:S(2)}) copy-start(u32[32]{0:T(128)} %constant.35) | copy-start | bytes 388
  42.4 90.3 %copy-start.2 = (f32[4,4608]{1,0:T(4,128)S(1)}, f32[4,4608]{1,0:T(4,128)}, u32[]{:S(2)}) copy-start(f32[4,4608]{1,0:T(4,128)} %param.13) | copy-start | bytes 221188
  42.4 90.3 %copy-start.3 = (f32[4,4608]{1,0:T(4,128)S(1)}, f32[4,4608]{1,0:T(4,128)}, u32[]{:S(2)}) copy-start(f32[4,4608]{1,0:T(4,128)} %param.14) | copy-start | bytes 221188
  42.5 90.3 %copy-start.4 = (f32[4,4608]{1,0:T(4,128)S(1)}, f32[4,4608]{1,0:T(4,128)}, u32[]{:S(2)}) copy-start(f32[4,4608]{1,0:T(4,128)} %param.15) | copy-start | bytes 221188
  42.5 91.1 %all-gather.3.cloned.1.call-start = ((), (), s32[]{:S(2)}) async-start(), calls=%async_computation.3 | async-start | bytes 1474560 | tf_op jit(solution)/shard_map/all_gather | solution.py:54
Sparse Core Ops, SparseCore 0:
  10.3 32.0 reduce-scatter.1
  44.7 31.0 all-reduce.2
  78.7 30.9 all-gather.2
where the time goes:
time: 143 us; the launch traced here: 142 us
  waiting for transfers between devices  68.4 us (48%)
  blocking collectives  52.8 us (37%)
  between operations  14.5 us (10%)
  other arithmetic  3.55 us (2%)
  local copies, waits for them, and re-layouts  3.1 us (2%)
    reduce_scatter x1, waiting for transfers between devices, local(): lax.psum_scatter(local_grads.astype(jnp.bfloat16), 'dp', scatter_dimensio...  34.4 us
    psum x1, waiting for transfers between devices, local(): lax.psum(partial_rows.astype(jnp.bfloat16), 'inst').astype(jnp.float32)  33.3 us
    unnamed x1, blocking collectives  20.5 us
    all_gather x1, blocking collectives, local(): lax.all_gather(gain_piece, 'dp', axis=0, tiled=True)  13.2 us
    psum x1, blocking collectives, local(): lax.psum(gain_piece.astype(jnp.bfloat16), 'inst').astype(jnp.float32)  10.9 us
    psum x1, blocking collectives, local(): gain_piece = lax.psum(gain_piece, 'tp')  8.21 us
    unnamed x18, local copies, waits for them, and re-layouts  3.08 us
  transfers between devices with their start and end apart: 3, of which 2 were waited for; matrix products, arithmetic and copies ran while one was open for 1% of the time, Pallas kernels for 0%

commit v1 on v0

--- a/solution.py
+++ b/solution.py
@@ -46,7 +46,9 @@
     )
     gradient, gain_piece = (
         lax.psum(partial_rows.astype(jnp.bfloat16), "inst").astype(jnp.float32),
-        lax.psum(gain_piece.astype(jnp.bfloat16), "inst").astype(jnp.float32),
+        jnp.sum(lax.all_gather(gain_piece.astype(jnp.bfloat16), "inst"), axis=0).astype(
+            jnp.float32
+        ),
     )
     kernel_master_new, kernel_first_new, kernel_second_new = adam_update(
         gradient, kernel_master, kernel_first, kernel_second

time: 143 us -> 137 us (0.958)
  blocking collectives: 52.8 us -> 47.2 us
    psum x1 -> x0, blocking collectives: 10.9 us -> none  [local(): lax.psum(gain_piece.astype(jnp.bfloat16), 'inst').astype(jnp.float32)]
    all_gather x0 -> x1, blocking collectives: none -> 5.26 us  [local(): lax.all_gather(gain_piece.astype(jnp.bfloat16), 'inst')]
    unnamed x18 -> x19, local copies, waits for them, and re-layouts: 3.08 us -> 3.09 us
where the time goes in v1:
time: 137 us
  waiting for transfers between devices  68.4 us (50%)
  blocking collectives  47.2 us (34%)
  between operations  14.5 us (11%)
  other arithmetic  3.65 us (3%)
  local copies, waits for them, and re-layouts  3.11 us (2%)
    reduce_scatter x1, waiting for transfers between devices, local(): lax.psum_scatter(local_grads.astype(jnp.bfloat16), 'dp', scatter_dimensio...  34.4 us
    psum x1, waiting for transfers between devices, local(): lax.psum(partial_rows.astype(jnp.bfloat16), 'inst').astype(jnp.float32)  33.3 us
    unnamed x1, blocking collectives  20.5 us
    all_gather x1, blocking collectives, local(): lax.all_gather(gain_piece, 'dp', axis=0, tiled=True)  13.2 us
    psum x1, blocking collectives, local(): gain_piece = lax.psum(gain_piece, 'tp')  8.22 us
    all_gather x1, blocking collectives, local(): lax.all_gather(gain_piece.astype(jnp.bfloat16), 'inst')  5.26 us
    unnamed x19, local copies, waits for them, and re-layouts  3.09 us
    convert_element_type x1, other arithmetic, local(): kernel_master_new.astype(jnp.bfloat16)  2.74 us
  transfers between devices with their start and end apart: 3, of which 2 were waited for; matrix products, arithmetic and copies ran while one was open for 1% of the time, Pallas kernels for 0%

profile of v1, /device:TPU:0, one launch (start us, length us, event | category | flops | bytes accessed | tf_op | source)
XLA Modules:
  0.0 136.9 jit_solution(10018656724080055523)
XLA Ops:
  7.2 0.0 copy-start.1
  7.2 0.0 copy-start
  7.2 0.0 reduce-scatter.2.cloned.1.call-start
  7.2 0.7 reduce-scatter.2.cloned.1.call-update
  7.9 0.0 all-reduce.3.cloned.1.call-start
  8.0 34.4 %reduce-scatter.2.cloned.1.call-done = bf16[1,32,4608]{2,1,0:T(8,128)(2,1)} async-done(((bf16[1,128,4608]{2,1,0:T(8,128)(2,1)}), bf16[1,32,4608]{2,1,0:T(8,128)(2,1)}) %reduce-scatter.2.cloned.1.call-update) | async-done | bytes 294928 | tf_op jit(solution)/shard_map/reduce_scatter | solution.py:40
  42.4 0.0 all-reduce.3.cloned.1.call-update
  42.4 0.0 copy-start.5
  42.4 0.0 copy-start.6
  42.5 0.0 all-gather.5.cloned.1.call-start
  42.5 33.3 %all-reduce.3.cloned.1.call-done = bf16[1,32,4608]{2,1,0:T(8,128)(2,1)} async-done(((bf16[1,32,4608]{2,1,0:T(8,128)(2,1)}), bf16[1,32,4608]{2,1,0:T(8,128)(2,1)}) %all-reduce.3.cloned.1.call-update) | async-done | bytes 294928 | tf_op jit(solution)/shard_map/psum | solution.py:48
  75.8 0.0 copy-done
  75.8 2.7 %fusion.7 = (bf16[1,32,4608]{2,1,0:T(8,128)(2,1)}, f32[1,32,4608]{2,1,0:T(8,128)}, f32[1,32,4608]{2,1,0:T(8,128)}, f32[1,32,4608]{2,1,0:T(8,128)}) fusion(f32[1,32,4608]{2,1,0:T(8,128)S(1)} %copy-done, bf16[1,32,4608]{2,1,0:T(8,128)(2,1)} %all-reduce.3.cloned.1.call-done, f32[1,32,4608]{2,1,0:T(8,128)S(1)} %copy-done.1, f32[1,32,4608]{2,1,0:T(8,128)} %param.11), kind=kLoop, calls=%fused_computation.11 | loop fusion | flops 2506752 | bytes 4128768 | tf_op jit(solution)/shard_map/convert_element_type | solution.py:56
  78.5 0.0 all-gather.5.cloned.1.call-update
  78.6 0.6 dynamic-slice
  79.9 20.5 %all-reduce = bf16[18432]{0:T(1024)(128)(2,1)S(1)} all-reduce(bf16[18432]{0:T(1024)(128)(2,1)S(1)} %squeeze.7), channel_id=4, replica_groups=mesh['inst'=4,'dp'=4,'tp'=2] {'dp'}, use_global_device_ids=true, to_apply=%region_2.0.clone | all-reduce | flops 18432 | bytes 73728
  100.4 0.1 dynamic-slice.1
  100.5 5.3 %all-gather.1 = bf16[4,1,4608]{2,1,0:T(2,128)(2,1)S(1)} all-gather(bf16[1,1,4608]{2,1,0:T(2,128)(2,1)S(1)} %reshape.23), channel_id=2, replica_groups=mesh['inst'=4,'dp'=4,'tp'=2] {'inst'}, dimensions={0}, use_global_device_ids=true | all-gather | bytes 46080 | tf_op jit(solution)/shard_map/all_gather | solution.py:49
  105.7 0.1 reduce_sum.12
  105.8 8.2 %psum.15 = f32[4608]{0:T(1024)S(1)} all-reduce(bf16[4608]{0:T(1024)(128)(2,1)S(1)} %reduce_sum.12), channel_id=1, replica_groups=mesh['inst'=4,'dp'=4,'tp'=2] {'tp'}, use_global_device_ids=true, to_apply=%region_4.0 | all-reduce | flops 4608 | bytes 27648 | tf_op jit(solution)/shard_map/psum | solution.py:57
  114.1 13.2 %all-gather.2 = f32[4,1,4608]{2,1,0:T(1,128)S(1)} all-gather(f32[1,1,4608]{2,1,0:T(1,128)S(1)} %reshape.25), channel_id=1, replica_groups=mesh['inst'=4,'dp'=4,'tp'=2] {'dp'}, dimensions={0}, use_global_device_ids=true | all-gather | bytes 92160 | tf_op jit(solution)/shard_map/all_gather | solution.py:58
  127.2 0.0 copy-done.4
  127.3 0.8 fusion.4
  128.1 2.4 %copy.23 = bf16[1,128,4608]{2,1,0:T(8,128)(2,1)} copy(bf16[1,128,4608]{2,1,0:T(8,128)(2,1)} %all-gather.5.cloned.1.call-done) | data formatting | bytes 2359296
  (12 shorter events, 0.1 us)
Async XLA Ops:
  7.2 68.6 %copy-start.1 = (f32[1,32,4608]{2,1,0:T(8,128)S(1)}, f32[1,32,4608]{2,1,0:T(8,128)}, u32[]{:S(2)}) copy-start(f32[1,32,4608]{2,1,0:T(8,128)} %param.10) | copy-start | bytes 1769476
  7.2 68.6 %copy-start = (f32[1,32,4608]{2,1,0:T(8,128)S(1)}, f32[1,32,4608]{2,1,0:T(8,128)}, u32[]{:S(2)}) copy-start(f32[1,32,4608]{2,1,0:T(8,128)} %param.9) | copy-start | bytes 1769476
  7.2 35.2 %reduce-scatter.2.cloned.1.call-start = ((), (), s32[]{:S(2)}) async-start(), calls=%async_computation.1 | async-start | bytes 1474560 | tf_op jit(solution)/shard_map/reduce_scatter | solution.py:40
  7.9 67.9 %all-reduce.3.cloned.1.call-start = ((), (), s32[]{:S(2)}) async-start(), calls=%async_computation.2 | async-start | bytes 589824 | tf_op jit(solution)/shard_map/psum | solution.py:48
  42.4 36.2 %copy-start.5 = (bf16[1,4,4608]{2,1,0:T(4,128)(2,1)S(1)}, bf16[1,4,4608]{2,1,0:T(4,128)(2,1)}, u32[]{:S(2)}) copy-start(bf16[1,4,4608]{2,1,0:T(4,128)(2,1)} %param.12) | copy-start | bytes 110596
  42.4 36.2 %copy-start.6 = (u32[32]{0:T(128)S(1)}, u32[32]{0:T(128)}, u32[]{:S(2)}) copy-start(u32[32]{0:T(128)} %constant.38) | copy-start | bytes 388
  42.4 84.8 %copy-start.2 = (f32[4,4608]{1,0:T(4,128)S(1)}, f32[4,4608]{1,0:T(4,128)}, u32[]{:S(2)}) copy-start(f32[4,4608]{1,0:T(4,128)} %param.13) | copy-start | bytes 221188
  42.4 84.8 %copy-start.3 = (f32[4,4608]{1,0:T(4,128)S(1)}, f32[4,4608]{1,0:T(4,128)}, u32[]{:S(2)}) copy-start(f32[4,4608]{1,0:T(4,128)} %param.14) | copy-start | bytes 221188
  42.5 84.8 %copy-start.4 = (f32[4,4608]{1,0:T(4,128)S(1)}, f32[4,4608]{1,0:T(4,128)}, u32[]{:S(2)}) copy-start(f32[4,4608]{1,0:T(4,128)} %param.15) | copy-start | bytes 221188
  42.5 85.6 %all-gather.5.cloned.1.call-start = ((), (), s32[]{:S(2)}) async-start(), calls=%async_computation.3 | async-start | bytes 1474560 | tf_op jit(solution)/shard_map/all_gather | solution.py:56
Sparse Core Ops, SparseCore 0:
  10.3 32.0 reduce-scatter.1
  44.7 31.0 all-reduce.2
  78.7 30.9 all-gather.4
